TPU v7x, 32 devices: a whole 2x2x4 slice. The times are simulated.
32 devices in a mesh: rows: 8 (over z, y), sub: 4 (over x, core).
Axes of the slice: x: 2, y: 2, z: 4, core: 2. Of those that a mesh axis runs over, the one named last changes fastest.
Arguments:
- frames: float32 [15, 32768], P(None, ('rows', 'sub')), may hold values from -1 to 1, as said below
- start_vector: float32 [3, 32768], P(None, ('rows', 'sub')), may hold values from -12 to 12
- edge_blocks: float32 [36, 65536], P(None, ('rows', 'sub')), may hold values from -14.4 to 14.4
- edge_source: int32 [32, 2048], P(('rows', 'sub')), may hold values from 0 to 1023
- edge_target: int32 [32, 2048], P(('rows', 'sub')), may hold values from 0 to 1535, as said below
- edge_count: int32 [32], P(('rows', 'sub')), may hold values from 1024 to 2048, as said below
- send_index: int32 [32, 512], P(('rows', 'sub')), may hold values from 0 to 1024, as said below
Outputs:
- new_frames: float32 [15, 32768], P(None, ('rows', 'sub'))
- last_vector: float32 [3, 32768], P(None, ('rows', 'sub'))
- tridiagonal: float32 [2, 4], replicated
Inputs may be any that keep to these rules, and one draw needn't show every extreme that they name: `frames`: each pose's block has orthonormal columns to float32 rounding. `edge_target`: below 1024: a pose of the same device. 1024 + u: halo slot u, whose block u // 16 on the providing device is never empty. `edge_count`: some device uses all 2048 slots. `send_index`: row q holds, in blocks of 16, the local poses that device q provides to device p (block p); a block is all poses or all 1024, which marks it empty; a device's block for itself is empty.
All inputs are finite; a program needn't handle non-finite values.
Results may differ from a plain program's by a relative error of at most 0.0003.
Values sent between devices are 32-bit elements; how exact they have to be, the bound alone decides.
A program may use at most 64 MiB of HBM per device.

v0:
```python
import jax
import jax.numpy as jnp
from jax import lax
from jax.sharding import PartitionSpec as P

RANK = 5
DIM = 3
LANCZOS = 4


polar_steps = 8
step_length = 0.3
epsilon = 1e-06


def symmetric(edge_blocks):
    blocks_six = edge_blocks.reshape(6, 6, -1)
    return 0.5 * (blocks_six + blocks_six.transpose(1, 0, 2))


def block_product(matrix, field_in):
    return jnp.sum(matrix[None, :, :, :] * field_in[:, None, :, :], axis=2)


def multiplier(left_field, right_field):
    product = jnp.sum(left_field[:, :, None, :] * right_field[:, None, :, :], axis=0)
    return 0.5 * (product + product.transpose(1, 0, 2))


def right_product(field_in, matrix):
    return jnp.sum(field_in[:, :, None, :] * matrix[None, :, :, :], axis=1)


def take_columns(table, index):
    return jnp.take(table, index, axis=1, mode="fill", fill_value=0.0)


def add_columns(values, index, width):
    total = jnp.zeros((values.shape[0], width), jnp.float32)
    return total.at[:, index].add(values, mode="drop")


def pack_rows(field_in, send_row):
    flattened = field_in.reshape(-1, field_in.shape[-1])
    return take_columns(flattened, send_row)


def return_rows(returned, send_row, poses_here):
    return add_columns(returned, send_row, poses_here)


def edge_terms(field_in, halo_vals, coupling, source, target, weight):
    copies = field_in.shape[0]
    poses_here = field_in.shape[2]
    edge_total = source.shape[0]
    extended = jnp.concatenate([field_in, halo_vals.reshape(copies, DIM, -1)], axis=2)
    full_width = extended.shape[2]
    values_first = take_columns(field_in.reshape(copies * DIM, poses_here), source).reshape(
        copies, DIM, edge_total
    )
    values_second = take_columns(extended.reshape(copies * DIM, full_width), target).reshape(
        copies, DIM, edge_total
    )
    upper_part = block_product(coupling[:3, :3], values_first) + block_product(
        coupling[:3, 3:], values_second
    )
    lower_part = block_product(coupling[3:, :3], values_first) + block_product(
        coupling[3:, 3:], values_second
    )
    upper_sum = add_columns(
        (upper_part * weight).reshape(copies * DIM, edge_total), source, poses_here
    )
    lower_sum = add_columns(
        (lower_part * weight).reshape(copies * DIM, edge_total), target, full_width
    )
    home_part = (upper_sum + lower_sum[:, :poses_here]).reshape(copies, DIM, poses_here)
    far_part = lower_sum[:, poses_here:].reshape(copies, DIM, full_width - poses_here)
    return (home_part, far_part)


def retract(frame_now, gradient, length):
    moved = frame_now - length * gradient
    norms = jnp.sum(moved * moved, axis=(0, 1))
    polar_now = moved * jnp.sqrt(DIM / norms)[None, None, :]
    identity = jnp.eye(DIM, dtype=jnp.float32)[:, :, None]
    for iteration in range(polar_steps):
        gram_matrix = jnp.sum(polar_now[:, :, None, :] * polar_now[:, None, :, :], axis=0)
        polar_now = right_product(polar_now, 1.5 * identity - 0.5 * gram_matrix)
    return polar_now


def on_device(frames, start_vector, edge_blocks, edge_source, edge_target, edge_count, send_index):
    poses_here = frames.shape[1]
    shards = lax.axis_size("rows") * lax.axis_size("sub")
    coupling = symmetric(edge_blocks)
    source = edge_source[0]
    target = edge_target[0]
    send_row = send_index[0]
    weight = (jnp.arange(source.shape[0], dtype=jnp.int32) < edge_count[0]).astype(jnp.float32)

    def split_product(field_in, halo_vals):
        return edge_terms(field_in, halo_vals, coupling, source, target, weight)

    frame_now = frames.reshape(RANK, DIM, poses_here)
    halo_vals = lax.all_to_all(
        pack_rows(frame_now, send_row), ("rows", "sub"), split_axis=1, concat_axis=1, tiled=True
    )
    near_part, far_part = split_product(frame_now, halo_vals)
    returned = lax.all_to_all(
        far_part.reshape(RANK * DIM, -1), ("rows", "sub"), split_axis=1, concat_axis=1, tiled=True
    )
    euclidean = near_part + return_rows(returned, send_row, poses_here).reshape(
        RANK, DIM, poses_here
    )
    multipliers = multiplier(frame_now, euclidean)
    gradient = 2.0 * (euclidean - right_product(frame_now, multipliers))
    total_square = lax.psum(jnp.sum(gradient * gradient), ("rows", "sub"))
    length = (
        step_length * jnp.sqrt(jnp.float32(poses_here * shards)) / jnp.sqrt(total_square + epsilon)
    )
    retracted = retract(frame_now, gradient, length)
    halo_moved = lax.all_to_all(
        pack_rows(retracted, send_row), ("rows", "sub"), split_axis=1, concat_axis=1, tiled=True
    )
    near_moved, far_moved = split_product(retracted, halo_moved)
    returned_moved = lax.all_to_all(
        far_moved.reshape(RANK * DIM, -1), ("rows", "sub"), split_axis=1, concat_axis=1, tiled=True
    )
    product_new = near_moved + return_rows(returned_moved, send_row, poses_here).reshape(
        RANK, DIM, poses_here
    )
    certificate_mult = multiplier(retracted, product_new)
    entries = DIM * poses_here * shards
    start_square = lax.psum(jnp.sum(start_vector * start_vector), ("rows", "sub"))
    start_field = start_vector.reshape(1, DIM, poses_here)
    krylov_basis = [start_field / jnp.sqrt(start_square / entries + epsilon)]
    alpha_list = []
    beta_list = []
    for iteration in range(LANCZOS):
        vector = krylov_basis[-1]
        halo_vector = lax.all_to_all(
            pack_rows(vector, send_row), ("rows", "sub"), split_axis=1, concat_axis=1, tiled=True
        )
        near_vector, far_vector = split_product(vector, halo_vector)
        returned_vector = lax.all_to_all(
            far_vector.reshape(DIM, -1), ("rows", "sub"), split_axis=1, concat_axis=1, tiled=True
        )
        image_vec = near_vector + return_rows(returned_vector, send_row, poses_here).reshape(
            1, DIM, poses_here
        )
        image_vec = image_vec - right_product(vector, certificate_mult)
        local_dots = jnp.stack([jnp.sum(member * image_vec) for member in krylov_basis])
        summed_dots, square_total = lax.psum(
            (local_dots, jnp.sum(image_vec * image_vec)), ("rows", "sub")
        )
        projected = summed_dots / entries
        for position in range(len(krylov_basis)):
            image_vec = image_vec - projected[position] * krylov_basis[position]
        beta_now = jnp.sqrt(square_total / entries - jnp.sum(projected * projected) + epsilon)
        krylov_basis.append(image_vec / beta_now)
        alpha_list.append(projected[-1])
        beta_list.append(beta_now)
    tridiagonal = jnp.stack([jnp.stack(alpha_list), jnp.stack(beta_list)])
    return (
        retracted.reshape(RANK * DIM, poses_here),
        krylov_basis[-1].reshape(DIM, poses_here),
        tridiagonal,
    )


def solution(mesh):
    in_specs = (
        P(None, ("rows", "sub")),
        P(None, ("rows", "sub")),
        P(None, ("rows", "sub")),
        P(("rows", "sub"), None),
        P(("rows", "sub"), None),
        P(("rows", "sub")),
        P(("rows", "sub"), None),
    )
    out_specs = (P(None, ("rows", "sub")), P(None, ("rows", "sub")), P())
    return jax.shard_map(
        on_device, mesh=mesh, in_specs=in_specs, out_specs=out_specs, check_vma=False
    )
```

profile of v0, /device:TPU:0, one launch (start us, length us, event | category | flops | bytes accessed | tf_op | source)
XLA Modules:
  0.0 608.0 jit_solution(1578713201348669233)
XLA Ops:
  4.7 7.3 %all-to-all-start = ((f32[32,1,240]{2,1,0:T(1,128)}), f32[32,1,240]{2,1,0:T(1,128)S(1)}, u32[]{:S(2)}, u32[]{:S(2)}) async-start(f32[32,1,240]{2,1,0:T(1,128)} %reshape.1031), calls=%async_computation | async-start | bytes 65536 | tf_op jit(solution)/shard_map/all_to_all | solution.py:105
  31.8 11.7 %scatter_custom_fusion = f32[15,1536]{0,1:T(8,128)S(1)} fusion(s32[2048]{0:T(1024)S(1)} %bitcast.201, f32[2048,15]{1,0:T(8,128)S(1)} %copy.377, f32[]{:T(128)} %constant.61.clone.1), kind=kCustom, calls=%fused_computation.68 | custom fusion | flops 30720 | bytes 92164 | tf_op jit(solution)/shard_map/scatter-add | solution.py:40
  44.3 5.8 all-to-all-start.1
  51.2 11.7 %scatter_fusion = f32[15,1024]{0,1:T(8,128)S(1)} fusion(f32[15,1024]{0,1:T(8,128)S(1)} %slice-done.1, s32[2048]{0:T(1024)S(1)} %bitcast.183, f32[2048,15]{1,0:T(8,128)S(1)} %copy.378), kind=kCustom, calls=%fused_computation.19 | custom fusion | flops 30720 | bytes 376832 | tf_op jit(solution)/shard_map/scatter-add | solution.py:40
  67.7 40.7 %all-reduce.4 = (f32[]{:T(128)}, f32[]{:T(128)}) all-reduce(f32[]{:T(128)} %get-tuple-element.95, f32[]{:T(128)} %multiply_reduce_fusion.63), channel_id=1, replica_groups=mesh['rows'=8,'sub'=4] {'rows','sub'}, use_global_device_ids=true, to_apply=%region_10.14 | all-reduce | flops 2 | bytes 16 | tf_op jit(solution)/shard_map/psum | solution.py:117
  154.3 11.8 %scatter_custom_fusion.3 = f32[3,1536]{0,1:T(8,128)S(1)} fusion(s32[2048]{0:T(1024)} %bitcast.202, f32[2048,3]{1,0:T(8,128)S(1)} %copy.389, f32[]{:T(128)} %constant.61.clone.1), kind=kCustom, calls=%fused_computation.64 | custom fusion | flops 6144 | bytes 18944 | tf_op jit(solution)/shard_map/scatter-add | solution.py:40
  167.0 6.4 %all-to-all-start.3 = ((f32[3,32,16]{2,0,1:T(4,128)}), f32[3,32,16]{2,0,1:T(4,128)}, u32[]{:S(2)}, u32[]{:S(2)}) async-start(f32[3,32,16]{2,0,1:T(4,128)} %copy.391), calls=%async_computation.3 | async-start | bytes 131072 | tf_op jit(solution)/shard_map/all_to_all | solution.py:145
  185.7 11.8 %scatter_custom_fusion.6 = f32[15,1536]{0,1:T(8,128)S(1)} fusion(s32[2048]{0:T(1024)} %bitcast.203, f32[2048,15]{1,0:T(8,128)S(1)} %copy.403, f32[]{:T(128)} %constant.61.clone.1), kind=kCustom, calls=%fused_computation.66 | custom fusion | flops 30720 | bytes 92672 | tf_op jit(solution)/shard_map/scatter-add | solution.py:40
  198.4 5.9 all-to-all-start.5
  206.2 11.7 %scatter_fusion.1 = f32[3,1024]{0,1:T(8,128)S(1)} fusion(f32[3,1024]{0,1:T(8,128)S(1)} %slice-done.3, s32[2048]{0:T(1024)S(1)} %bitcast.184, f32[2048,3]{1,0:T(8,128)S(1)} %copy.390), kind=kCustom, calls=%fused_computation.22 | custom fusion | flops 6144 | bytes 81920 | tf_op jit(solution)/shard_map/scatter-add | solution.py:40
  222.9 11.8 %scatter_fusion.2 = f32[15,1024]{0,1:T(8,128)S(1)} fusion(f32[15,1024]{0,1:T(8,128)S(1)} %slice-done, s32[2048]{0:T(1024)S(1)} %bitcast.185, f32[2048,15]{1,0:T(8,128)S(1)} %copy.404), kind=kCustom, calls=%fused_computation.25 | custom fusion | flops 30720 | bytes 376832 | tf_op jit(solution)/shard_map/scatter-add | solution.py:40
  240.7 40.7 %all-reduce.3 = (f32[]{:T(128)}, f32[1]{0:T(128)}) all-reduce(f32[]{:T(128)} %get-tuple-element.72, f32[1]{0:T(128)} %bitcast.41), channel_id=1, replica_groups=mesh['rows'=8,'sub'=4] {'rows','sub'}, use_global_device_ids=true, to_apply=%region_49.56 | all-reduce | flops 2 | bytes 16 | tf_op jit(solution)/shard_map/psum | solution.py:153
  297.7 6.7 %all-to-all-done.6 = f32[3,32,16]{2,0,1:T(4,128)S(1)} async-done(((f32[3,32,16]{2,0,1:T(4,128)}), f32[3,32,16]{2,0,1:T(4,128)S(1)}, u32[]{:S(2)}, u32[]{:S(2)}) %all-to-all-start.6) | async-done | bytes 6176 | tf_op jit(solution)/shard_map/all_to_all | solution.py:141
  312.5 11.8 %scatter_custom_fusion.9 = f32[3,1536]{0,1:T(8,128)S(1)} fusion(s32[2048]{0:T(1024)} %bitcast.204, f32[2048,3]{1,0:T(8,128)S(1)} %copy.414, f32[]{:T(128)} %constant.61.clone.1), kind=kCustom, calls=%fused_computation.62 | custom fusion | flops 6144 | bytes 18944 | tf_op jit(solution)/shard_map/scatter-add | solution.py:40
  328.9 11.9 %scatter_fusion.3 = f32[3,1024]{0,1:T(8,128)S(1)} fusion(f32[3,1024]{0,1:T(8,128)S(1)} %slice-done.4, s32[2048]{0:T(1024)S(1)} %bitcast.186, f32[2048,3]{1,0:T(8,128)S(1)} %copy.415), kind=kCustom, calls=%fused_computation.28 | custom fusion | flops 6144 | bytes 81920 | tf_op jit(solution)/shard_map/scatter-add | solution.py:40
  346.0 40.7 %all-reduce.2 = (f32[]{:T(128)}, f32[2]{0:T(128)S(1)}) all-reduce(f32[]{:T(128)} %get-tuple-element.69, f32[2]{0:T(128)S(1)} %pad_maximum_fusion.3), channel_id=1, replica_groups=mesh['rows'=8,'sub'=4] {'rows','sub'}, use_global_device_ids=true, to_apply=%region_62.69 | all-reduce | flops 3 | bytes 24 | tf_op jit(solution)/shard_map/psum | solution.py:153
  403.8 6.7 %all-to-all-done.8 = f32[3,32,16]{2,0,1:T(4,128)S(1)} async-done(((f32[3,32,16]{2,0,1:T(4,128)}), f32[3,32,16]{2,0,1:T(4,128)S(1)}, u32[]{:S(2)}, u32[]{:S(2)}) %all-to-all-start.8) | async-done | bytes 6176 | tf_op jit(solution)/shard_map/all_to_all | solution.py:141
  417.8 11.8 %scatter_custom_fusion.12 = f32[3,1536]{0,1:T(8,128)S(1)} fusion(s32[2048]{0:T(1024)} %bitcast.205, f32[2048,3]{1,0:T(8,128)S(1)} %copy.428, f32[]{:T(128)} %constant.61.clone.1), kind=kCustom, calls=%fused_computation.60 | custom fusion | flops 6144 | bytes 18944 | tf_op jit(solution)/shard_map/scatter-add | solution.py:40
  434.2 11.7 %scatter_fusion.4 = f32[3,1024]{0,1:T(8,128)S(1)} fusion(f32[3,1024]{0,1:T(8,128)S(1)} %slice-done.5, s32[2048]{0:T(1024)S(1)} %bitcast.187, f32[2048,3]{1,0:T(8,128)S(1)} %copy.429), kind=kCustom, calls=%fused_computation.31 | custom fusion | flops 6144 | bytes 81920 | tf_op jit(solution)/shard_map/scatter-add | solution.py:40
  451.9 40.7 %all-reduce.1 = (f32[]{:T(128)}, f32[3]{0:T(128)S(1)}) all-reduce(f32[]{:T(128)} %get-tuple-element.65, f32[3]{0:T(128)S(1)} %pad_maximum_fusion.4), channel_id=1, replica_groups=mesh['rows'=8,'sub'=4] {'rows','sub'}, use_global_device_ids=true, to_apply=%region_77.84 | all-reduce | flops 4 | bytes 32 | tf_op jit(solution)/shard_map/psum | solution.py:153
  510.2 6.7 %all-to-all-done.10 = f32[3,32,16]{2,0,1:T(4,128)S(1)} async-done(((f32[3,32,16]{2,0,1:T(4,128)}), f32[3,32,16]{2,0,1:T(4,128)S(1)}, u32[]{:S(2)}, u32[]{:S(2)}) %all-to-all-start.10) | async-done | bytes 6176 | tf_op jit(solution)/shard_map/all_to_all | solution.py:141
  524.2 11.8 %scatter_custom_fusion.15 = f32[3,1536]{0,1:T(8,128)S(1)} fusion(s32[2048]{0:T(1024)} %bitcast.206, f32[2048,3]{1,0:T(8,128)S(1)} %copy.442, f32[]{:T(128)} %constant.61.clone.1), kind=kCustom, calls=%fused_computation.58 | custom fusion | flops 6144 | bytes 18944 | tf_op jit(solution)/shard_map/scatter-add | solution.py:40
  540.6 11.7 %scatter_fusion.5 = f32[3,1024]{0,1:T(8,128)S(1)} fusion(f32[3,1024]{0,1:T(8,128)S(1)} %slice-done.2, s32[2048]{0:T(1024)S(1)} %bitcast.188, f32[2048,3]{1,0:T(8,128)S(1)} %copy.443), kind=kCustom, calls=%fused_computation.34 | custom fusion | flops 6144 | bytes 81920 | tf_op jit(solution)/shard_map/scatter-add | solution.py:40
  558.6 40.7 %all-reduce = (f32[]{:T(128)}, f32[4]{0:T(128)S(1)}) all-reduce(f32[]{:T(128)} %get-tuple-element.60, f32[4]{0:T(128)S(1)} %pad_maximum_fusion.5), channel_id=1, replica_groups=mesh['rows'=8,'sub'=4] {'rows','sub'}, use_global_device_ids=true, to_apply=%region_93.100 | all-reduce | flops 5 | bytes 40 | tf_op jit(solution)/shard_map/psum | solution.py:153
  (394 shorter events, 206.1 us)
Async XLA Ops:
  2.5 118.3 %copy-start.45 = (s32[1024]{0:T(1024)}, s32[1024]{0:T(1024)S(1)}, u32[]{:S(2)}) copy-start(s32[1024]{0:T(1024)S(1)} %pad_clamp_fusion) | copy-start | bytes 12292
  3.7 9.9 %copy-start.34 = (f32[36,2048]{1,0:T(8,128)S(1)}, f32[36,2048]{1,0:T(8,128)}, u32[]{:S(2)}) copy-start(f32[36,2048]{1,0:T(8,128)} %param.21) | copy-start | bytes 884740
  4.7 17.5 %all-to-all-start = ((f32[32,1,240]{2,1,0:T(1,128)}), f32[32,1,240]{2,1,0:T(1,128)S(1)}, u32[]{:S(2)}, u32[]{:S(2)}) async-start(f32[32,1,240]{2,1,0:T(1,128)} %reshape.1031), calls=%async_computation | async-start | bytes 65536 | tf_op jit(solution)/shard_map/all_to_all | solution.py:105
  12.8 101.0 %copy-start.30 = (s32[2048]{0:T(1024)}, s32[2048]{0:T(1024)S(1)}, u32[]{:S(2)}) copy-start(s32[2048]{0:T(1024)S(1)} %fusion.27) | copy-start | bytes 24580
  13.5 18.3 %copy-start.54 = (s32[2048,1]{0,1:T(1,128)}, s32[2048,1]{0,1:T(1,128)S(1)}, u32[]{:S(2)}) copy-start(s32[2048,1]{0,1:T(1,128)S(1)} %compare_select_fusion.1) | copy-start | bytes 24580
  13.5 10.7 %copy-start.22 = (s32[2048]{0:T(1024)}, s32[2048]{0:T(1024)S(1)}, u32[]{:S(2)}) copy-start(s32[2048]{0:T(1024)S(1)} %fusion.28) | copy-start | bytes 24580
  13.6 16.1 %copy-start.37 = (pred[2048]{0:T(1024)(128)(4,1)}, pred[2048]{0:T(1024)(128)(4,1)S(1)}, u32[]{:S(2)}) copy-start(pred[2048]{0:T(1024)(128)(4,1)S(1)} %compare_and_fusion) | copy-start | bytes 6148
  13.6 37.0 %copy-start.20 = (s32[2048,1]{0,1:T(1,128)}, s32[2048,1]{0,1:T(1,128)S(1)}, u32[]{:S(2)}) copy-start(s32[2048,1]{0,1:T(1,128)S(1)} %compare_select_fusion) | copy-start | bytes 24580
  13.6 50.4 %copy-start.55 = (s32[512,1]{0,1:T(1,128)}, s32[512,1]{0,1:T(1,128)S(1)}, u32[]{:S(2)}) copy-start(s32[512,1]{0,1:T(1,128)S(1)} %compare_select_fusion.4) | copy-start | bytes 6148
  14.0 16.4 %copy-start.7 = (f32[3,3,2048]{2,1,0:T(4,128)}, f32[3,3,2048]{2,1,0:T(4,128)S(1)}, u32[]{:S(2)}) copy-start(f32[3,3,2048]{2,1,0:T(4,128)S(1)} %get-tuple-element.97) | copy-start | bytes 221188
  14.0 16.4 %copy-start.9 = (f32[3,3,2048]{2,1,0:T(4,128)}, f32[3,3,2048]{2,1,0:T(4,128)S(1)}, u32[]{:S(2)}) copy-start(f32[3,3,2048]{2,1,0:T(4,128)S(1)} %get-tuple-element.98) | copy-start | bytes 221188
  44.3 18.8 %all-to-all-start.1 = ((f32[32,1,240]{2,1,0:T(1,128)}), f32[32,1,240]{2,1,0:T(1,128)S(1)}, u32[]{:S(2)}, u32[]{:S(2)}) async-start(f32[32,1,240]{2,1,0:T(1,128)} %reshape.1033), calls=%async_computation.1 | async-start | bytes 65536 | tf_op jit(solution)/shard_map/all_to_all | solution.py:109
  130.0 12.2 %all-to-all-start.2 = ((f32[3,32,16]{2,0,1:T(4,128)}), f32[3,32,16]{2,0,1:T(4,128)}, u32[]{:S(2)}, u32[]{:S(2)}) async-start(f32[3,32,16]{2,0,1:T(4,128)} %copy.385), calls=%async_computation.2 | async-start | bytes 131072 | tf_op jit(solution)/shard_map/all_to_all | solution.py:141
  142.2 24.8 %all-to-all-start.4 = ((f32[32,1,240]{2,1,0:T(1,128)}), f32[32,1,240]{2,1,0:T(1,128)S(1)}, u32[]{:S(2)}, u32[]{:S(2)}) async-start(f32[32,1,240]{2,1,0:T(1,128)} %reshape.1035), calls=%async_computation.4 | async-start | bytes 65536 | tf_op jit(solution)/shard_map/all_to_all | solution.py:122
  166.1 38.3 %copy-start.3 = (f32[3,1536]{0,1:T(8,128)}, f32[3,1536]{0,1:T(8,128)S(1)}, u32[]{:S(2)}) copy-start(f32[3,1536]{0,1:T(8,128)S(1)} %scatter_custom_fusion.3) | copy-start | bytes 55300
  167.0 31.4 %all-to-all-start.3 = ((f32[3,32,16]{2,0,1:T(4,128)}), f32[3,32,16]{2,0,1:T(4,128)}, u32[]{:S(2)}, u32[]{:S(2)}) async-start(f32[3,32,16]{2,0,1:T(4,128)} %copy.391), calls=%async_computation.3 | async-start | bytes 131072 | tf_op jit(solution)/shard_map/all_to_all | solution.py:145
  197.5 24.4 %copy-start = (f32[15,1536]{0,1:T(8,128)}, f32[15,1536]{0,1:T(8,128)S(1)}, u32[]{:S(2)}) copy-start(f32[15,1536]{0,1:T(8,128)S(1)} %scatter_custom_fusion.6) | copy-start | bytes 276484
  198.4 36.4 %all-to-all-start.5 = ((f32[32,1,240]{2,1,0:T(1,128)}), f32[32,1,240]{2,1,0:T(1,128)S(1)}, u32[]{:S(2)}, u32[]{:S(2)}) async-start(f32[32,1,240]{2,1,0:T(1,128)} %reshape.1037), calls=%async_computation.5 | async-start | bytes 65536 | tf_op jit(solution)/shard_map/all_to_all | solution.py:126
  292.3 12.1 %all-to-all-start.6 = ((f32[3,32,16]{2,0,1:T(4,128)}), f32[3,32,16]{2,0,1:T(4,128)S(1)}, u32[]{:S(2)}, u32[]{:S(2)}) async-start(f32[3,32,16]{2,0,1:T(4,128)} %copy.410), calls=%async_computation.6 | async-start | bytes 131072 | tf_op jit(solution)/shard_map/all_to_all | solution.py:141
  325.2 15.8 %all-to-all-start.7 = ((f32[3,32,16]{2,0,1:T(4,128)}), f32[3,32,16]{2,0,1:T(4,128)S(1)}, u32[]{:S(2)}, u32[]{:S(2)}) async-start(f32[3,32,16]{2,0,1:T(4,128)} %copy.416), calls=%async_computation.7 | async-start | bytes 131072 | tf_op jit(solution)/shard_map/all_to_all | solution.py:145
  398.5 12.1 %all-to-all-start.8 = ((f32[3,32,16]{2,0,1:T(4,128)}), f32[3,32,16]{2,0,1:T(4,128)S(1)}, u32[]{:S(2)}, u32[]{:S(2)}) async-start(f32[3,32,16]{2,0,1:T(4,128)} %copy.424), calls=%async_computation.8 | async-start | bytes 131072 | tf_op jit(solution)/shard_map/all_to_all | solution.py:141
  430.5 15.5 %all-to-all-start.9 = ((f32[3,32,16]{2,0,1:T(4,128)}), f32[3,32,16]{2,0,1:T(4,128)S(1)}, u32[]{:S(2)}, u32[]{:S(2)}) async-start(f32[3,32,16]{2,0,1:T(4,128)} %copy.430), calls=%async_computation.9 | async-start | bytes 131072 | tf_op jit(solution)/shard_map/all_to_all | solution.py:145
  504.9 12.0 %all-to-all-start.10 = ((f32[3,32,16]{2,0,1:T(4,128)}), f32[3,32,16]{2,0,1:T(4,128)S(1)}, u32[]{:S(2)}, u32[]{:S(2)}) async-start(f32[3,32,16]{2,0,1:T(4,128)} %copy.438), calls=%async_computation.10 | async-start | bytes 131072 | tf_op jit(solution)/shard_map/all_to_all | solution.py:141
  536.9 15.5 %all-to-all-start.11 = ((f32[3,32,16]{2,0,1:T(4,128)}), f32[3,32,16]{2,0,1:T(4,128)S(1)}, u32[]{:S(2)}, u32[]{:S(2)}) async-start(f32[3,32,16]{2,0,1:T(4,128)} %copy.444), calls=%async_computation.11 | async-start | bytes 131072 | tf_op jit(solution)/shard_map/all_to_all | solution.py:145
  (50 other events, 115.0 us)
where the time goes:
time: 619 us; the launch traced here: 608 us
  blocking collectives  204 us (33%)
  other arithmetic  195 us (32%)
  local copies, waits for them, and re-layouts  120 us (19%)
  starting transfers between devices  54.6 us (9%)
  waiting for transfers between devices  23.9 us (4%)
  between operations  11.7 us (2%)
    psum x4, blocking collectives, on_device(): lax.psum((local_dots, jnp.sum(image_vec * image_vec)), ('rows', 'sub'))  163 us
    scatter-add x18, other arithmetic, add_columns(): return total.at[:, index].add(values, mode='drop')  156 us
    gather x18, local copies, waits for them, and re-layouts, take_columns(): return jnp.take(table, index, axis=1, mode='fill', fill_value=0.0)  73 us
    psum x1, blocking collectives, on_device(): total_square = lax.psum(jnp.sum(gradient * gradient), ('rows', 'sub'))  40.7 us
    all_to_all x4, waiting for transfers between devices, on_device(): lax.all_to_all(pack_rows(vector, send_row), ('rows', 'sub'), split_axis=1...  23.9 us
    all_to_all x4, starting transfers between devices, on_device(): lax.all_to_all(pack_rows(vector, send_row), ('rows', 'sub'), split_axis=1...  18.9 us
    unnamed x121, local copies, waits for them, and re-layouts  14.4 us
    all_to_all x4, starting transfers between devices, on_device(): lax.all_to_all(far_vector.reshape(DIM, -1), ('rows', 'sub'), split_axis=1...  14.1 us
  transfers between devices with their start and end apart: 12, of which 4 were waited for; matrix products, arithmetic and copies ran while one was open for 22% of the time, Pallas kernels for 0%

commit v1 on v0

v1 whole, which is shorter than its diff:
```python
import functools

import jax
import jax.numpy as jnp
from jax import lax
from jax.experimental import pallas as pl
from jax.experimental.pallas import tpu as pltpu
from jax.sharding import PartitionSpec as P

RANK = 5
DIM = 3
LANCZOS = 4
LANES = 128
CHUNK = 256
EXCHANGES = 5 + 2 * (LANCZOS - 1) + 1

polar_steps = 8
step_length = 0.3
epsilon = 1e-06

F32 = jnp.float32
BF16 = jnp.bfloat16
MESH = pl.DeviceIdType.MESH


def split_three(x):
    high = x.astype(BF16).astype(F32)
    rest = x - high
    middle = rest.astype(BF16).astype(F32)
    low = rest - middle
    parts = [high, middle, low, jnp.zeros((8, x.shape[1]), F32)]
    return jnp.concatenate(parts, axis=0).astype(BF16)


def fold(y, rows):
    return (y[2 * rows:3 * rows] + y[rows:2 * rows]) + y[:rows]


def dot_nn(a, b):
    return lax.dot_general(a, b, (((1,), (0,)), ((), ())), preferred_element_type=F32)


def dot_nt(a, b):
    return lax.dot_general(a, b, (((1,), (1,)), ((), ())), preferred_element_type=F32)


def total(x):
    return jnp.sum(jnp.sum(x, axis=1, keepdims=True), axis=0, keepdims=True)


def column_sum(x):
    return jnp.sum(x, axis=0, keepdims=True)


def multiplier(left, right):
    raw = [[column_sum(left[d] * right[e]) for e in range(DIM)] for d in range(DIM)]
    return [[0.5 * (raw[d][e] + raw[e][d]) for e in range(DIM)] for d in range(DIM)]


def right_product(field, matrix):
    return [sum(field[d] * matrix[d][e] for d in range(DIM)) for e in range(DIM)]


def kernel(
    shards, sub_size,
    frames, start, blocks, source, target, count, send_index,
    new_frames, last_vector, tridiagonal,
    src_hot, dst_hot, send_hot, coupling, near_first, near_second,
    x_split, h_split, up_split, lo_split, stage, result, send, recv,
    send_sem, recv_sem,
):
    poses = frames.shape[1]
    edges = source.shape[1]
    halo = send_index.shape[1]
    slots = halo // shards
    per = LANES // slots
    lane_blocks = halo // LANES
    row_me, sub_me = lax.axis_index("rows"), lax.axis_index("sub")
    me = row_me * sub_size + sub_me
    entries = float(DIM * poses * shards)

    def peer_of(i):
        peer = lax.rem(me + i, shards)
        return peer, (peer // sub_size, lax.rem(peer, sub_size))

    barrier = pltpu.get_barrier_semaphore()

    @pl.loop(1, shards)
    def _(i):
        pl.semaphore_signal(barrier, inc=1, device_id=peer_of(i)[1], device_id_type=MESH)

    def hot(ref, index, rows):
        step = 32
        width = index.shape[1]
        row = lax.broadcasted_iota(jnp.int32, (step, width), 0)

        @pl.loop(0, rows // step)
        def _(r):
            shifted = index - r * step
            ref[pl.ds(pl.multiple_of(r * step, step), step), :] = jnp.where(
                row == shifted, 1.0, 0.0
            ).astype(BF16)

    lane = lax.broadcasted_iota(jnp.int32, (8, LANES), 1)
    group = lane // slots
    sub_row = lax.broadcasted_iota(jnp.int32, (8, LANES), 0)
    scalar_base = DIM * slots

    def scalar_tile(scalars):
        tile = jnp.zeros((8, LANES), F32)
        for k, value in enumerate(scalars):
            tile = jnp.where((lane == scalar_base + k) & (sub_row == 0), value, tile)
        return tile

    def blocks_loop(body):
        lax.fori_loop(0, lane_blocks, lambda b, c: (body(b), c)[1], 0, unroll=lane_blocks <= 4)

    def post(ex, tiles, scalars):
        extra = scalar_tile(scalars)

        def one(b):
            for j in range(per):
                message = extra
                for t in range(tiles):
                    part = stage[b, 8 * t:8 * t + 8, :]
                    shift = ((t - j) * slots) % LANES
                    part = pltpu.roll(part, shift, 1) if shift else part
                    message = jnp.where(group == t, part, message)
                send[ex, b * per + j] = message

        blocks_loop(one)
        recv[ex, me] = send[ex, me]

        @pl.loop(1, shards)
        def _(i):
            peer, where = peer_of(i)
            pltpu.make_async_remote_copy(
                src_ref=send.at[ex, peer],
                dst_ref=recv.at[ex, me],
                send_sem=send_sem.at[ex],
                recv_sem=recv_sem.at[ex],
                device_id=where,
                device_id_type=MESH,
            ).start()

    def arrive(ex):
        whole = recv.at[ex, pl.ds(0, shards - 1)]
        pltpu.make_async_copy(whole, whole, recv_sem.at[ex]).wait()

    def unpack(ex, tiles):
        def one(b):
            for t in range(tiles):
                value = jnp.zeros((8, LANES), F32)
                for j in range(per):
                    shift = ((j - t) * slots) % LANES
                    part = recv[ex, b * per + j]
                    part = pltpu.roll(part, shift, 1) if shift else part
                    value = jnp.where(group == j, part, value)
                stage[b, 8 * t:8 * t + 8, :] = value

        blocks_loop(one)
        rows = 8 * tiles
        return jnp.concatenate([stage[b, :rows, :] for b in range(lane_blocks)], axis=1)

    def arrived_scalars(ex, number):
        tile = jnp.sum(recv[ex], axis=0)
        return [
            total(jnp.where((lane == scalar_base + k) & (sub_row == 0), tile, 0.0))
            for k in range(number)
        ]

    def stage_field(value, rows, c):
        for k in range(CHUNK // LANES):
            stage[c * (CHUNK // LANES) + k, :rows, :] = value[:, k * LANES:(k + 1) * LANES]

    def chunk_of(c):
        return pl.ds(pl.multiple_of(c * CHUNK, CHUNK), CHUNK)

    def product(x, tiles, ex, scalars, before=None):
        rows = 8 * tiles
        used = 3 * rows + 8
        single = tiles == 1
        x_split[:used, :] = split_three(x)

        @pl.loop(0, halo // CHUNK)
        def _(c):
            value = fold(dot_nn(x_split[:used, :], send_hot[:, chunk_of(c)]), rows)
            stage_field(value, rows, c)

        if before is not None:
            pl.semaphore_wait(barrier, shards - 1)
        post(ex, tiles, scalars)
        if before is not None:
            before()

        @pl.loop(0, edges // CHUNK)
        def _(c):
            at = chunk_of(c)
            near_first[:rows, at] = fold(dot_nn(x_split[:used, :], src_hot[:, at]), rows)
            near_second[:rows, at] = fold(dot_nn(x_split[:used, :], dst_hot[:poses, at]), rows)

        arrive(ex)
        h_split[:used, :] = split_three(unpack(ex, tiles))

        @pl.loop(0, edges // CHUNK)
        def _(c):
            at = chunk_of(c)
            first = near_first[:rows, at]
            second = near_second[:rows, at] + fold(
                dot_nn(h_split[:used, :], dst_hot[poses:, at]), rows
            )
            if single:
                ends = [first[d:d + 1] for d in range(DIM)] + [second[d:d + 1] for d in range(DIM)]
                both = sum(coupling[8 * j:8 * j + 8, at] * ends[j] for j in range(6))
                up_split[:used, at] = split_three(both)
            else:
                ends = [first[8 * d:8 * d + 8] for d in range(DIM)] + [
                    second[8 * d:8 * d + 8] for d in range(DIM)
                ]
                both = [
                    sum(coupling[8 * j + i:8 * j + i + 1, at] * ends[j] for j in range(6))
                    for i in range(6)
                ]
                up_split[:used, at] = split_three(jnp.concatenate(both[:3], axis=0))
                lo_split[:used, at] = split_three(jnp.concatenate(both[3:], axis=0))

        upper = up_split
        lower = up_split if single else lo_split

        def lowered(y):
            return pltpu.roll(y, 8 - DIM, 0) if single else y

        @pl.loop(0, halo // CHUNK)
        def _(c):
            at = pl.ds(pl.multiple_of(poses + c * CHUNK, CHUNK), CHUNK)
            stage_field(lowered(fold(dot_nt(lower[:used, :], dst_hot[at, :]), rows)), rows, c)

        post(ex + 1, tiles, [])

        @pl.loop(0, poses // CHUNK)
        def _(c):
            at = chunk_of(c)
            result[:rows, at] = fold(dot_nt(upper[:used, :], src_hot[at, :]), rows) + lowered(
                fold(dot_nt(lower[:used, :], dst_hot[at, :]), rows)
            )

        arrive(ex + 1)
        h_split[:used, :] = split_three(unpack(ex + 1, tiles))

        @pl.loop(0, poses // CHUNK)
        def _(c):
            at = chunk_of(c)
            result[:rows, at] += fold(dot_nt(h_split[:used, :], send_hot[at, :]), rows)

        return result[:rows, :], arrived_scalars(ex, len(scalars))

    def summed(ex, scalars):
        post(ex, 0, scalars)
        arrive(ex)
        return arrived_scalars(ex, len(scalars))

    hot(send_hot, send_index[...], poses)

    frame_now = []
    padding = jnp.zeros((8 - RANK, poses), F32)
    for d in range(DIM):
        rows = [frames[3 * a + d:3 * a + d + 1, :] for a in range(RANK)]
        frame_now.append(jnp.concatenate(rows + [padding], axis=0))
    vector = [start[d:d + 1, :] for d in range(DIM)]
    copy_row = lax.broadcasted_iota(jnp.int32, (8, poses), 0)

    def build():
        hot(src_hot, source[...], poses)
        hot(dst_hot, target[...], poses + halo)
        live = lax.broadcasted_iota(jnp.int32, (1, edges), 1) < count[...]
        weight = jnp.where(live, 0.5, 0.0)
        for j in range(6):
            for i in range(6):
                a, b = 6 * i + j, 6 * j + i
                coupling[8 * j + i:8 * j + i + 1, :] = weight * (
                    blocks[a:a + 1, :] + blocks[b:b + 1, :]
                )
            coupling[8 * j + 6:8 * j + 8, :] = jnp.zeros((2, edges), F32)

    def stacked(parts):
        return jnp.concatenate(parts, axis=0)

    square = sum(total(v * v) for v in vector)
    joint = stacked([jnp.where(copy_row == RANK, vector[d], frame_now[d]) for d in range(DIM)])
    image, (start_square,) = product(joint, DIM, 0, [square], before=build)
    euclidean = [image[8 * d:8 * d + 8] for d in range(DIM)]
    start_scale = 1.0 / jnp.sqrt(start_square / entries + epsilon)
    start_image = [euclidean[d][RANK:RANK + 1] * start_scale for d in range(DIM)]
    krylov = [[v * start_scale for v in vector]]

    projected = right_product(frame_now, multiplier(frame_now, euclidean))
    gradient = [
        jnp.where(copy_row < RANK, 2.0 * (euclidean[d] - projected[d]), 0.0) for d in range(DIM)
    ]
    (square,) = summed(2, [sum(total(g * g) for g in gradient)])
    length = step_length * (float(poses * shards) ** 0.5) / jnp.sqrt(square + epsilon)
    moved = [frame_now[d] - length * gradient[d] for d in range(DIM)]
    norms = column_sum(sum(m * m for m in moved))
    scale = jnp.sqrt(DIM / norms)
    polar = [m * scale for m in moved]
    for _ in range(polar_steps):
        gram = [[None] * DIM for _ in range(DIM)]
        for d in range(DIM):
            for e in range(d, DIM):
                value = -0.5 * column_sum(polar[d] * polar[e])
                gram[d][e] = gram[e][d] = value + 1.5 if d == e else value
        polar = right_product(polar, gram)
    for d in range(DIM):
        for a in range(RANK):
            new_frames[3 * a + d:3 * a + d + 1, :] = polar[d][a:a + 1]

    image, _ = product(stacked(polar), DIM, 3, [])
    certificate = multiplier(polar, [image[8 * d:8 * d + 8] for d in range(DIM)])

    def certify(image_rows, vec):
        back = right_product(vec, certificate)
        return [image_rows[d] - back[d] for d in range(DIM)]

    images = [certify(start_image, krylov[0])]
    alphas, betas = [], []
    for k in range(LANCZOS):
        current = images[-1]
        dots = [
            total(sum(member[d] * current[d] for d in range(DIM))) for member in krylov
        ] + [total(sum(c * c for c in current))]
        ex = 5 + 2 * k
        if k < LANCZOS - 1:
            rows = stacked(current + [jnp.zeros((8 - DIM, poses), F32)])
            image, sums = product(rows, 1, ex, dots)
            following = certify([image[d:d + 1] for d in range(DIM)], current)
        else:
            sums = summed(ex, dots)
        weights = [s / entries for s in sums[:-1]]
        beta = jnp.sqrt(sums[-1] / entries - sum(h * h for h in weights) + epsilon)
        inverse = 1.0 / beta
        krylov.append([
            (current[d] - sum(h * q[d] for h, q in zip(weights, krylov))) * inverse
            for d in range(DIM)
        ])
        if k < LANCZOS - 1:
            images.append([
                (following[d] - sum(h * w[d] for h, w in zip(weights, images))) * inverse
                for d in range(DIM)
            ])
        alphas.append(weights[-1])
        betas.append(beta)
    for d in range(DIM):
        last_vector[d:d + 1, :] = krylov[-1][d]
    column = lax.broadcasted_iota(jnp.int32, (2, LANCZOS), 1)
    line = lax.broadcasted_iota(jnp.int32, (2, LANCZOS), 0)
    table = jnp.zeros((2, LANCZOS), F32)
    for k in range(LANCZOS):
        table = jnp.where(column == k, jnp.where(line == 0, alphas[k], betas[k]), table)
    tridiagonal[...] = table

    for ex in range(EXCHANGES):
        whole = send.at[ex, pl.ds(0, shards - 1)]
        pltpu.make_async_copy(whole, whole, send_sem.at[ex]).wait()


def on_device(shards, sub_size, frames, start, blocks, source, target, count, send_index):
    poses = frames.shape[1]
    edges = source.shape[1]
    halo = send_index.shape[1]
    vmem = pl.BlockSpec(memory_space=pltpu.VMEM)
    split_rows = 3 * 8 * DIM + 8
    return pl.pallas_call(
        functools.partial(kernel, shards, sub_size),
        out_shape=(
            jax.ShapeDtypeStruct((RANK * DIM, poses), F32),
            jax.ShapeDtypeStruct((DIM, poses), F32),
            jax.ShapeDtypeStruct((2, LANCZOS), F32),
        ),
        in_specs=[vmem] * 7,
        out_specs=(vmem, vmem, vmem),
        scratch_shapes=[
            pltpu.VMEM((poses, edges), BF16),
            pltpu.VMEM((poses + halo, edges), BF16),
            pltpu.VMEM((poses, halo), BF16),
            pltpu.VMEM((48, edges), F32),
            pltpu.VMEM((8 * DIM, edges), F32),
            pltpu.VMEM((8 * DIM, edges), F32),
            pltpu.VMEM((split_rows, poses), BF16),
            pltpu.VMEM((split_rows, halo), BF16),
            pltpu.VMEM((split_rows, edges), BF16),
            pltpu.VMEM((split_rows, edges), BF16),
            pltpu.VMEM((halo // LANES, 8 * DIM, LANES), F32),
            pltpu.VMEM((8 * DIM, poses), F32),
            pltpu.VMEM((EXCHANGES, shards, 8, LANES), F32),
            pltpu.VMEM((EXCHANGES, shards, 8, LANES), F32),
            pltpu.SemaphoreType.DMA((EXCHANGES,)),
            pltpu.SemaphoreType.DMA((EXCHANGES,)),
        ],
        compiler_params=pltpu.CompilerParams(
            collective_id=0, has_side_effects=True, vmem_limit_bytes=60 * 1024 * 1024
        ),
    )(frames, start, blocks, source, target, count.reshape(1, 1), send_index)


def solution(mesh):
    shards = mesh.shape["rows"] * mesh.shape["sub"]
    in_specs = (
        P(None, ("rows", "sub")),
        P(None, ("rows", "sub")),
        P(None, ("rows", "sub")),
        P(("rows", "sub"), None),
        P(("rows", "sub"), None),
        P(("rows", "sub")),
        P(("rows", "sub"), None),
    )
    out_specs = (P(None, ("rows", "sub")), P(None, ("rows", "sub")), P())
    return jax.shard_map(
        functools.partial(on_device, shards, mesh.shape["sub"]),
        mesh=mesh,
        in_specs=in_specs,
        out_specs=out_specs,
        check_vma=False,
    )
```

time: 619 us -> 101 us (0.16); the launches traced: 608 us -> 101 us
  blocking collectives: 204 us -> 0 us
  other arithmetic: 195 us -> 0 us
  local copies, waits for them, and re-layouts: 120 us -> 2.7 us
  Pallas kernels: 0 us -> 96.8 us
  starting transfers between devices: 54.6 us -> 0 us
  waiting for transfers between devices: 23.9 us -> 0 us
  between operations: 11.7 us -> 1.3 us
    psum x5 -> x0, blocking collectives: 204 us -> none  [the longest x4 163 us: on_device(): lax.psum((local_dots, jnp.sum(image_vec * image_vec)), ('rows', 'sub'))]
    scatter-add x18 -> x0, other arithmetic: 156 us -> none  [add_columns(): return total.at[:, index].add(values, mode='drop')]
    pallas_call x0 -> x1, Pallas kernels: none -> 96.8 us  [on_device(): pl.pallas_call(functools.partial(kernel, shards, sub_size), out_shape=(ja...]
    gather x18 -> x0, local copies, waits for them, and re-layouts: 73 us -> none  [take_columns(): return jnp.take(table, index, axis=1, mode='fill', fill_value=0.0)]
    all_to_all x12 -> x0, starting transfers between devices: 54.6 us -> none  [the longest x4 18.9 us: on_device(): lax.all_to_all(pack_rows(vector, send_row), ('rows', 'sub'), split_axis=1...]
    all_to_all x12 -> x0, waiting for transfers between devices: 23.9 us -> none  [the longest x4 23.9 us: on_device(): lax.all_to_all(pack_rows(vector, send_row), ('rows', 'sub'), split_axis=1...]
    unnamed x121 -> x7, local copies, waits for them, and re-layouts: 14.4 us -> 2.7 us
    all_to_all x29 -> x0, local copies, waits for them, and re-layouts: 10.9 us -> none  [the longest x16 5.34 us: on_device(): lax.all_to_all(far_vector.reshape(DIM, -1), ('rows', 'sub'), split_axis=1...]
  transfers between devices with their start and end apart: 12 -> 0, of which waited for: 4 -> 0; matrix products, arithmetic and copies ran while one was open for 22% -> 0% of each run, Pallas kernels for 0% -> 0%
where the time goes in v1:
time: 101 us
  Pallas kernels  96.8 us (96%)
  local copies, waits for them, and re-layouts  2.7 us (3%)
  between operations  1.3 us (1%)
    pallas_call x1, Pallas kernels, on_device(): pl.pallas_call(functools.partial(kernel, shards, sub_size), out_shape=(ja...  96.8 us
    unnamed x7, local copies, waits for them, and re-layouts  2.7 us

profile of v1, /device:TPU:0, one launch (start us, length us, event | category | flops | bytes accessed | tf_op | source)
XLA Modules:
  0.0 100.8 jit_solution(15064600624163428486)
XLA Ops:
  1.3 96.8 %shard_map.94 = (f32[15,1024]{1,0:T(8,128)}, f32[3,1024]{1,0:T(4,128)}, f32[2,4]{1,0:T(2,128)}) custom-call(f32[15,1024]{1,0:T(8,128)} %frames.1, f32[3,1024]{1,0:T(4,128)} %start.1, f32[36,2048]{1,0:T(8,128)} %blocks.1, s32[1,2048]{1,0:T(1,128)} %source.1, s32[1,2048]{1,0:T(1,128)} %target.1, s32[1,1]{1,0:T(1,128)} %bitcast.1.count, s32[1,512]{1,0:T(1,128)} %send_index.1), custom_call_target="tpu_custom_call" | custom-call | tf_op jit(solution)/shard_map/pallas_call | solution.py:372
  98.1 0.0 copy-start
  98.1 1.5 %copy.14 = f32[15,1024]{1,0:T(8,128)} copy(f32[15,1024]{1,0:T(8,128)} %get-tuple-element.6) | data formatting | bytes 122880
  99.6 0.0 copy-done
  99.6 0.0 copy-start.1
  99.6 0.6 copy.15
  100.2 0.1 copy-done.1
  100.2 0.6 copy.16
Async XLA Ops:
  98.1 1.5 %copy-start = (f32[3,1024]{1,0:T(4,128)S(1)}, f32[3,1024]{1,0:T(4,128)}, u32[]{:S(2)}) copy-start(f32[3,1024]{1,0:T(4,128)} %get-tuple-element.7) | copy-start | bytes 36868
  99.6 0.7 copy-start.1

commit v2 on v1

--- a/solution.py
+++ b/solution.py
@@ -11,7 +11,8 @@
 DIM = 3
 LANCZOS = 4
 LANES = 128
-CHUNK = 256
+CHUNK = 1024
+ROWS = {0: 1, 1: 4, DIM: 8}
 EXCHANGES = 5 + 2 * (LANCZOS - 1) + 1
 
 polar_steps = 8
@@ -20,6 +21,7 @@
 
 F32 = jnp.float32
 BF16 = jnp.bfloat16
+F8 = jnp.float8_e4m3fn
 MESH = pl.DeviceIdType.MESH
 
 
@@ -99,7 +101,7 @@
             shifted = index - r * step
             ref[pl.ds(pl.multiple_of(r * step, step), step), :] = jnp.where(
                 row == shifted, 1.0, 0.0
-            ).astype(BF16)
+            ).astype(F8)
 
     lane = lax.broadcasted_iota(jnp.int32, (8, LANES), 1)
     group = lane // slots
@@ -128,23 +130,27 @@
                     message = jnp.where(group == t, part, message)
                 send[ex, b * per + j] = message
 
-        blocks_loop(one)
-        recv[ex, me] = send[ex, me]
+        if tiles:
+            blocks_loop(one)
+            recv[ex, me] = send[ex, me]
+        else:
+            send[ex, 0] = extra
+            recv[ex, me] = extra
 
         @pl.loop(1, shards)
         def _(i):
             peer, where = peer_of(i)
             pltpu.make_async_remote_copy(
-                src_ref=send.at[ex, peer],
-                dst_ref=recv.at[ex, me],
+                src_ref=send.at[ex, peer if tiles else 0, pl.ds(0, ROWS[tiles])],
+                dst_ref=recv.at[ex, me, pl.ds(0, ROWS[tiles])],
                 send_sem=send_sem.at[ex],
                 recv_sem=recv_sem.at[ex],
                 device_id=where,
                 device_id_type=MESH,
             ).start()
 
-    def arrive(ex):
-        whole = recv.at[ex, pl.ds(0, shards - 1)]
+    def arrive(ex, tiles):
+        whole = recv.at[ex, pl.ds(0, shards - 1), pl.ds(0, ROWS[tiles])]
         pltpu.make_async_copy(whole, whole, recv_sem.at[ex]).wait()
 
     def unpack(ex, tiles):
@@ -163,18 +169,20 @@
         return jnp.concatenate([stage[b, :rows, :] for b in range(lane_blocks)], axis=1)
 
     def arrived_scalars(ex, number):
-        tile = jnp.sum(recv[ex], axis=0)
+        tile = jnp.sum(recv[ex, :, 0:1, :], axis=0)
         return [
-            total(jnp.where((lane == scalar_base + k) & (sub_row == 0), tile, 0.0))
+            jnp.sum(jnp.where(lane[:1] == scalar_base + k, tile, 0.0), axis=1, keepdims=True)
             for k in range(number)
         ]
 
     def stage_field(value, rows, c):
-        for k in range(CHUNK // LANES):
-            stage[c * (CHUNK // LANES) + k, :rows, :] = value[:, k * LANES:(k + 1) * LANES]
-
-    def chunk_of(c):
-        return pl.ds(pl.multiple_of(c * CHUNK, CHUNK), CHUNK)
+        for k in range(halo_chunk // LANES):
+            stage[c * (halo_chunk // LANES) + k, :rows, :] = value[:, k * LANES:(k + 1) * LANES]
+
+    halo_chunk = min(CHUNK, halo)
+
+    def chunk_of(c, size=CHUNK):
+        return pl.ds(pl.multiple_of(c * size, size), size)
 
     def product(x, tiles, ex, scalars, before=None):
         rows = 8 * tiles
@@ -182,9 +190,9 @@
         single = tiles == 1
         x_split[:used, :] = split_three(x)
 
-        @pl.loop(0, halo // CHUNK)
-        def _(c):
-            value = fold(dot_nn(x_split[:used, :], send_hot[:, chunk_of(c)]), rows)
+        @pl.loop(0, halo // halo_chunk)
+        def _(c):
+            value = fold(dot_nn(x_split[:used, :], send_hot[:, chunk_of(c, halo_chunk)]), rows)
             stage_field(value, rows, c)
 
         if before is not None:
@@ -199,7 +207,7 @@
             near_first[:rows, at] = fold(dot_nn(x_split[:used, :], src_hot[:, at]), rows)
             near_second[:rows, at] = fold(dot_nn(x_split[:used, :], dst_hot[:poses, at]), rows)
 
-        arrive(ex)
+        arrive(ex, tiles)
         h_split[:used, :] = split_three(unpack(ex, tiles))
 
         @pl.loop(0, edges // CHUNK)
@@ -230,9 +238,9 @@
         def lowered(y):
             return pltpu.roll(y, 8 - DIM, 0) if single else y
 
-        @pl.loop(0, halo // CHUNK)
-        def _(c):
-            at = pl.ds(pl.multiple_of(poses + c * CHUNK, CHUNK), CHUNK)
+        @pl.loop(0, halo // halo_chunk)
+        def _(c):
+            at = pl.ds(pl.multiple_of(poses + c * halo_chunk, halo_chunk), halo_chunk)
             stage_field(lowered(fold(dot_nt(lower[:used, :], dst_hot[at, :]), rows)), rows, c)
 
         post(ex + 1, tiles, [])
@@ -244,7 +252,7 @@
                 fold(dot_nt(lower[:used, :], dst_hot[at, :]), rows)
             )
 
-        arrive(ex + 1)
+        arrive(ex + 1, tiles)
         h_split[:used, :] = split_three(unpack(ex + 1, tiles))
 
         @pl.loop(0, poses // CHUNK)
@@ -256,7 +264,7 @@
 
     def summed(ex, scalars):
         post(ex, 0, scalars)
-        arrive(ex)
+        arrive(ex, 0)
         return arrived_scalars(ex, len(scalars))
 
     hot(send_hot, send_index[...], poses)
@@ -358,8 +366,10 @@
         table = jnp.where(column == k, jnp.where(line == 0, alphas[k], betas[k]), table)
     tridiagonal[...] = table
 
+    tiles_of = [DIM, DIM, 0, DIM, DIM] + [1] * (2 * (LANCZOS - 1)) + [0]
     for ex in range(EXCHANGES):
-        whole = send.at[ex, pl.ds(0, shards - 1)]
+        rows = ROWS[tiles_of[ex]]
+        whole = send.at[ex, pl.ds(0, shards - 1), pl.ds(0, rows)]
         pltpu.make_async_copy(whole, whole, send_sem.at[ex]).wait()
 
 
@@ -379,9 +389,9 @@
         in_specs=[vmem] * 7,
         out_specs=(vmem, vmem, vmem),
         scratch_shapes=[
-            pltpu.VMEM((poses, edges), BF16),
-            pltpu.VMEM((poses + halo, edges), BF16),
-            pltpu.VMEM((poses, halo), BF16),
+            pltpu.VMEM((poses, edges), F8),
+            pltpu.VMEM((poses + halo, edges), F8),
+            pltpu.VMEM((poses, halo), F8),
             pltpu.VMEM((48, edges), F32),
             pltpu.VMEM((8 * DIM, edges), F32),
             pltpu.VMEM((8 * DIM, edges), F32),

time: 101 us -> 82.5 us (0.82)
  Pallas kernels: 96.8 us -> 78.3 us
    pallas_call x1, Pallas kernels: 96.8 us -> 78.3 us  [on_device(): pl.pallas_call(functools.partial(kernel, shards, sub_size), out_shape=(ja...]
where the time goes in v2:
time: 82.5 us; the launch traced here: 82.3 us
  Pallas kernels  78.3 us (95%)
  local copies, waits for them, and re-layouts  2.7 us (3%)
  between operations  1.3 us (2%)
    pallas_call x1, Pallas kernels, on_device(): pl.pallas_call(functools.partial(kernel, shards, sub_size), out_shape=(ja...  78.3 us
    unnamed x7, local copies, waits for them, and re-layouts  2.7 us

profile of v2, /device:TPU:0, one launch (start us, length us, event | category | flops | bytes accessed | tf_op | source)
XLA Modules:
  0.0 82.3 jit_solution(15138809579640424022)
XLA Ops:
  1.3 78.3 %shard_map.94 = (f32[15,1024]{1,0:T(8,128)}, f32[3,1024]{1,0:T(4,128)}, f32[2,4]{1,0:T(2,128)}) custom-call(f32[15,1024]{1,0:T(8,128)} %frames.1, f32[3,1024]{1,0:T(4,128)} %start.1, f32[36,2048]{1,0:T(8,128)} %blocks.1, s32[1,2048]{1,0:T(1,128)} %source.1, s32[1,2048]{1,0:T(1,128)} %target.1, s32[1,1]{1,0:T(1,128)} %bitcast.1.count, s32[1,512]{1,0:T(1,128)} %send_index.1), custom_call_target="tpu_custom_call" | custom-call | tf_op jit(solution)/shard_map/pallas_call | solution.py:382
  79.6 0.0 copy-start
  79.6 1.5 %copy.14 = f32[15,1024]{1,0:T(8,128)} copy(f32[15,1024]{1,0:T(8,128)} %get-tuple-element.6) | data formatting | bytes 122880
  81.1 0.0 copy-done
  81.1 0.0 copy-start.1
  81.1 0.6 copy.15
  81.7 0.1 copy-done.1
  81.7 0.6 copy.16
Async XLA Ops:
  79.6 1.5 %copy-start = (f32[3,1024]{1,0:T(4,128)S(1)}, f32[3,1024]{1,0:T(4,128)}, u32[]{:S(2)}) copy-start(f32[3,1024]{1,0:T(4,128)} %get-tuple-element.7) | copy-start | bytes 36868
  81.1 0.7 copy-start.1
